TPU v7x, 32 devices: a whole 2x2x4 slice. The times are simulated.
32 devices in a mesh: site: 8 (over z, x), clade: 4 (over y, core).
Axes of the slice: x: 2, y: 2, z: 4, core: 2. Of those that a mesh axis runs over, the one named last changes fastest.
Arguments:
- tips: int32 [128, 32768], P('clade', 'site'), may hold values from 0 to 4
- transition: float32 [248, 4, 4, 4], P('clade'), may hold values from 0 to 1, as said below
- clade_children: int32 [124, 2], P('clade'), may hold values from 0 to 61, as said below
- upper_transition: float32 [6, 4, 4, 4], replicated, may hold values from 0 to 1, as said below
- upper_children: int32 [3, 2], replicated, may hold values from 0 to 5, as said below
- pattern_weights: int32 [32768], P('site'), may hold values from 1 to 8
Outputs:
- weighted_loglik: float32 [32768], P(('site', 'clade'))
- mean_loglik: float32 [], replicated
Inputs may be any that keep to these rules, and one draw needn't show every extreme that they name: `tips`: code 4 marks a gap or an unknown base. `transition`: every row of every 4 x 4 block is positive and sums to 1. `upper_transition`: every row of every 4 x 4 block is positive and sums to 1. `clade_children`: rows k * (31) to (k + 1) * 31 - 1 belong to clade k; its row j holds two different node numbers below 32 + j, and each node 0 to 61 of the clade is a child in exactly one row of the clade. `upper_children`: row j holds two different node numbers below 4 + j, and each node 0 to 5 is a child in exactly one row.
All inputs are finite; a program needn't handle non-finite values.
Results may differ from a plain program's by a relative error of at most 0.0003.
Values sent between devices are 32-bit elements; how exact they have to be, the bound alone decides.
A program may use at most 64 MiB of HBM per device.

v0:
```python
import functools

import jax
import jax.numpy as jnp
from jax import lax
from jax.experimental import pallas as pl
from jax.experimental.pallas import tpu as pltpu
from jax.sharding import PartitionSpec as P

MESH = pl.DeviceIdType.MESH


def tree_max(values):
    while len(values) > 1:
        paired = [jnp.maximum(a, b) for a, b in zip(values[::2], values[1::2])]
        values = paired + ([values[-1]] if len(values) % 2 else [])
    return values[0]


def tree_sum(values):
    while len(values) > 1:
        paired = [a + b for a, b in zip(values[::2], values[1::2])]
        values = paired + ([values[-1]] if len(values) % 2 else [])
    return values[0]


def kernel(dims, tips_in, matrices_in, children_in, upper_in, upper_children_in, weights_in,
           weighted, mean, tips, matrices, children, upper, upper_children, weights, load, branch, row_sum, upper_branch, moved, root, held,
           sums_clade, sums_site, root_send, root_recv, clade_send, clade_recv, site_send, site_recv):
    leaves, rates, rows, clades, sites_axis = dims
    entries = rates * 4
    size = entries * 4
    inner = leaves - 1
    piece = rows // clades
    half_clades = clades // 2
    half_rows = rows // 2
    width = half_rows // 8
    me = lax.axis_index("clade")
    block = lax.axis_index("site")
    my_half = me // half_clades
    my_low = me % half_clades

    def tips_copy(turn):
        half = lax.rem(my_half + 1 + turn, 2)
        return pltpu.make_async_copy(
            tips_in.at[:, pl.ds(half * (half_rows * 8), half_rows * 8), :], tips.at[turn], load.at[turn])

    loads = [pltpu.make_async_copy(source, target, load.at[2 + k]) for k, (source, target) in enumerate([
        (matrices_in, matrices), (upper_in, upper), (children_in, children),
        (upper_children_in, upper_children), (weights_in, weights)])]
    loads[0].start()
    tips_copy(0).start()
    for copy in loads[1:]:
        copy.start()
    tips_copy(1).start()

    barrier = pltpu.get_barrier_semaphore()
    for step in range(1, clades):
        pl.semaphore_signal(barrier, inc=1, device_id={"clade": lax.rem(me + step, clades)}, device_id_type=MESH)
    for step in range(1, sites_axis):
        pl.semaphore_signal(barrier, inc=1, device_id={"site": lax.rem(block + step, sites_axis)}, device_id_type=MESH)

    def lay_out(node):
        branch[node * size:(node + 1) * size, :] = jnp.broadcast_to(matrices[:, node:node + 1], (size, 128))

    loads[0].wait()
    totals = tree_sum([matrices[pl.ds(b, entries, stride=4), :] for b in range(4)])
    def lay_out_tip(node):
        lay_out(node)
        row_sum[node * entries:(node + 1) * entries, :] = jnp.broadcast_to(totals[:, node:node + 1], (entries, 128))
    loads[1].wait()
    for node in range(2 * clades - 2):
        upper_branch[node * size:(node + 1) * size, :] = jnp.broadcast_to(upper[:, node:node + 1], (size, 128))

    def spread(ref, row, count=8):
        return jnp.broadcast_to(ref[pl.ds(row, 1), :], (count, 128))

    def merge(left, right):
        product = [a * b for a, b in zip(left, right)]
        biggest = tree_max(product)
        inverse = 1.0 / biggest
        return [p * inverse for p in product], jnp.log(biggest)

    def transform(ref, base, parts, store):
        count = parts[0][0].shape[0]
        for rate in range(rates):
            for state in range(4):
                entry = rate * 4 + state
                acc = None
                for b in range(4):
                    weight = spread(ref, base + entry * 4 + b, count)
                    terms = [weight * part[rate * 4 + b] for part in parts]
                    acc = terms if acc is None else [x + y for x, y in zip(acc, terms)]
                for w, value in enumerate(acc):
                    store(entry, w, value)

    root_copies = []
    for turn in range(2):
        half = lax.rem(my_half + 1 + turn, 2)

        def tip(i, carry):
            codes = [tips[turn, i // 8, pl.ds(w * 64 + i % 8, 8, stride=8), :] for w in range(width)]
            is_code = [[code == b for b in range(4)] for code in codes]
            for entry in range(entries):
                probs = [spread(branch, i * size + entry * 4 + b) for b in range(4)]
                total = spread(row_sum, i * entries + entry)
                for w in range(width):
                    value = total
                    for b in range(4):
                        value = jnp.where(is_code[w][b], probs[b], value)
                    moved[i * entries + entry, w * 8:(w + 1) * 8, :] = value
            return carry

        tips_copy(turn).wait()
        if turn == 0:
            for i in range(2):
                lay_out_tip(i)
            for i in range(leaves):
                if i + 2 < leaves:
                    lay_out_tip(i + 2)
                if i < inner - 1:
                    lay_out(leaves + i)
                tip(i, 0)
            for copy in loads[2:]:
                copy.wait()
        else:
            lax.fori_loop(0, leaves, tip, 0, unroll=2)

        def merged(j, scale):
            c = children[0, j]
            d = children[1, j]
            parts, scales = [], []
            for w in range(width):
                window = slice(w * 8, (w + 1) * 8)
                part, log_m = merge([moved[c * entries + e, window, :] for e in range(entries)],
                                    [moved[d * entries + e, window, :] for e in range(entries)])
                parts.append(part)
                scales.append(scale[w] + log_m)
            return parts, tuple(scales)

        def advance(j, scale):
            parts, scale = merged(j, scale)
            node = leaves + j

            def store(entry, w, value):
                moved[node * entries + entry, w * 8:(w + 1) * 8, :] = value

            transform(branch, node * size, parts, store)
            return scale

        scale = tuple(jnp.zeros((8, 128), jnp.float32) for _ in range(width))
        scale = lax.fori_loop(0, inner - 1, advance, scale)
        parts, scale = merged(inner - 1, scale)
        first = half * half_clades

        def store_root(entry, w, value):
            for k in range(8 // piece if piece < 8 else 1):
                row = w * 8 + k * piece
                if piece >= 8:
                    root[first + row // piece, entry, row % piece:row % piece + 8, :] = value
                else:
                    root[first + row // piece, entry, :, :] = value[k * piece:(k + 1) * piece, :]

        transform(upper_branch, me * size, parts, store_root)
        for w in range(width):
            store_root(entries, w, scale[w])

        if turn == 0:
            pl.semaphore_wait(barrier, clades - 1 + sites_axis - 1)
        for step in range(turn, half_clades):
            target = half * half_clades + lax.rem(my_low + step, half_clades)
            slot = turn * half_clades + step
            copy = pltpu.make_async_remote_copy(
                src_ref=root.at[target], dst_ref=held.at[me],
                send_sem=root_send.at[slot], recv_sem=root_recv.at[slot],
                device_id={"clade": target}, device_id_type=MESH)
            copy.start()
            root_copies.append(copy)

    held[me] = root[me]
    for copy in root_copies:
        copy.wait_recv()

    scale = tree_sum([held[k, entries] for k in range(clades)])
    for j in range(clades - 1):
        c = upper_children[0, j]
        d = upper_children[1, j]
        part, log_m = merge([held[c, e] for e in range(entries)], [held[d, e] for e in range(entries)])
        scale = scale + log_m
        if j < clades - 2:
            def store_upper(entry, w, value):
                held[clades + j, entry, :, :] = value

            transform(upper_branch, (clades + j) * size, [part], store_upper)
    summed = tree_sum(part) / (4.0 * rates)
    value = weights[me].astype(jnp.float32) * (jnp.log(summed) + scale) / float(leaves * clades)
    weighted[...] = value

    def exchange(axis, index, count, sums, send, recv, mine):
        sums[index] = mine
        copies = []
        for step in range(1, count):
            copy = pltpu.make_async_remote_copy(
                src_ref=sums.at[index], dst_ref=sums.at[index],
                send_sem=send.at[step], recv_sem=recv.at[step],
                device_id={axis: lax.rem(index + step, count)}, device_id_type=MESH)
            copy.start()
            copies.append(copy)
        for copy in copies:
            copy.wait_recv()
        return copies, tree_sum([sums[k] for k in range(count)])

    copies, total = exchange("clade", me, clades, sums_clade, clade_send, clade_recv,
                             jnp.sum(value, axis=0, keepdims=True))
    root_copies += copies
    copies, total = exchange("site", block, sites_axis, sums_site, site_send, site_recv, total)
    root_copies += copies
    mean[0] = jnp.sum(total) / float(rows * 128 * sites_axis)
    for copy in root_copies:
        copy.wait_send()


def per_device(tips, transition, clade_children, upper_transition, upper_children, pattern_weights):
    leaves, sites = tips.shape
    rates = transition.shape[1]
    clades = lax.axis_size("clade")
    sites_axis = lax.axis_size("site")
    rows = sites // 128
    piece = rows // clades
    entries = rates * 4
    size = entries * 4
    nodes = 2 * leaves - 2
    codes = tips.reshape(leaves // 8, 8, rows, 128).transpose(0, 2, 1, 3).reshape(leaves // 8, rows * 8, 128)
    matrices = transition.transpose(1, 2, 3, 0).reshape(size, nodes)
    upper = upper_transition.transpose(1, 2, 3, 0).reshape(size, 2 * clades - 2)
    vmem = pl.BlockSpec(memory_space=pltpu.VMEM)
    smem = pl.BlockSpec(memory_space=pltpu.SMEM)
    weighted, mean = pl.pallas_call(
        functools.partial(kernel, (leaves, rates, rows, clades, sites_axis)),
        out_shape=(jax.ShapeDtypeStruct((piece, 128), jnp.float32), jax.ShapeDtypeStruct((1,), jnp.float32)),
        in_specs=[pl.BlockSpec(memory_space=pltpu.HBM)] * 6,
        out_specs=(vmem, smem),
        scratch_shapes=[
            pltpu.VMEM((2, leaves // 8, rows * 4, 128), jnp.int32),
            pltpu.VMEM((size, nodes), jnp.float32),
            pltpu.SMEM((2, leaves - 1), jnp.int32),
            pltpu.VMEM((size, 2 * clades - 2), jnp.float32),
            pltpu.SMEM((2, clades - 1), jnp.int32),
            pltpu.VMEM((clades, piece, 128), jnp.int32),
            pltpu.SemaphoreType.DMA((7,)),
            pltpu.VMEM((nodes * size, 128), jnp.float32),
            pltpu.VMEM((leaves * entries, 128), jnp.float32),
            pltpu.VMEM(((2 * clades - 2) * size, 128), jnp.float32),
            pltpu.VMEM((nodes * entries, rows // 2, 128), jnp.float32),
            pltpu.VMEM((clades, entries + 1, piece, 128), jnp.float32),
            pltpu.VMEM((2 * clades - 2, entries + 1, piece, 128), jnp.float32),
            pltpu.VMEM((clades, 1, 128), jnp.float32),
            pltpu.VMEM((sites_axis, 1, 128), jnp.float32),
            pltpu.SemaphoreType.DMA((clades,)),
            pltpu.SemaphoreType.DMA((clades,)),
            pltpu.SemaphoreType.DMA((clades,)),
            pltpu.SemaphoreType.DMA((clades,)),
            pltpu.SemaphoreType.DMA((sites_axis,)),
            pltpu.SemaphoreType.DMA((sites_axis,)),
        ],
        compiler_params=pltpu.CompilerParams(
            collective_id=0, has_side_effects=True, vmem_limit_bytes=67043328),
    )(codes, matrices, clade_children.T, upper, upper_children.T, pattern_weights.reshape(clades, piece, 128))
    return weighted.reshape(sites // clades), mean.reshape(())


def solution(mesh):
    placed = (
        P("clade", "site"),
        P("clade", None, None, None),
        P("clade", None),
        P(),
        P(),
        P("site"),
    )
    return jax.shard_map(
        per_device,
        mesh=mesh,
        in_specs=placed,
        out_specs=(P(("site", "clade")), P()),
        check_vma=False,
    )
```

profile of v0, /device:TPU:0, one launch (start us, length us, event | category | flops | bytes accessed | tf_op | source)
XLA Modules:
  0.0 22.8 jit_solution(12488467443631800069)
XLA Ops:
  0.6 19.1 %shard_map.77 = (f32[8,128]{1,0:T(8,128)}, f32[1]{0:T(128)}) custom-call(s32[4,256,128]{2,1,0:T(8,128)} %bitcast.16, f32[64,62]{1,0:T(8,128)} %bitcast.17, s32[2,31]{1,0:T(2,128)} %bitcast.21, f32[64,6]{1,0:T(8,128)} %bitcast.18, s32[2,3]{1,0:T(2,128)} %bitcast.22, s32[4,8,128]{2,1,0:T(8,128)} %bitcast.19), custom_call_target="tpu_custom_call" | custom-call | tf_op jit(solution)/shard_map/pallas_call | solution.py:238
  19.7 0.0 copy-start
  19.8 0.7 %copy-done = f32[8,128]{1,0:T(8,128)S(1)} copy-done((f32[8,128]{1,0:T(8,128)S(1)}, f32[8,128]{1,0:T(8,128)}, u32[]{:S(2)}) %copy-start) | copy-done | bytes 4120
  20.4 0.6 %copy.10 = f32[1024]{0:T(1024)} copy(f32[1024]{0:T(1024)S(1)} %bitcast.20) | data formatting | bytes 8192
Async XLA Ops:
  19.7 0.7 %copy-start = (f32[8,128]{1,0:T(8,128)S(1)}, f32[8,128]{1,0:T(8,128)}, u32[]{:S(2)}) copy-start(f32[8,128]{1,0:T(8,128)} %get-tuple-element.4) | copy-start | bytes 12292
where the time goes:
time: 23 us; the launch traced here: 22.8 us
  Pallas kernels  19.1 us (83%)
  between operations  2.41 us (10%)
  local copies, waits for them, and re-layouts  1.26 us (5%)
    pallas_call x1, Pallas kernels, per_device(): pl.pallas_call(functools.partial(kernel, (leaves, rates, rows, clades, si...  19.1 us
    unnamed x3, local copies, waits for them, and re-layouts  1.26 us

commit v1 on v0

--- a/solution.py
+++ b/solution.py
@@ -26,7 +26,7 @@
 
 def kernel(dims, tips_in, matrices_in, children_in, upper_in, upper_children_in, weights_in,
            weighted, mean, tips, matrices, children, upper, upper_children, weights, load, branch, row_sum, upper_branch, moved, root, held,
-           sums_clade, sums_site, root_send, root_recv, clade_send, clade_recv, site_send, site_recv):
+           sums, root_send, root_recv, sum_send, sum_recv):
     leaves, rates, rows, clades, sites_axis = dims
     entries = rates * 4
     size = entries * 4
@@ -55,10 +55,16 @@
     tips_copy(1).start()
 
     barrier = pltpu.get_barrier_semaphore()
-    for step in range(1, clades):
-        pl.semaphore_signal(barrier, inc=1, device_id={"clade": lax.rem(me + step, clades)}, device_id_type=MESH)
-    for step in range(1, sites_axis):
-        pl.semaphore_signal(barrier, inc=1, device_id={"site": lax.rem(block + step, sites_axis)}, device_id_type=MESH)
+    devices = clades * sites_axis
+    mine = block * clades + me
+
+    def greet(step, carry):
+        other = lax.rem(mine + step, devices)
+        pl.semaphore_signal(barrier, inc=1, device_id={"site": other // clades, "clade": lax.rem(other, clades)},
+                            device_id_type=MESH)
+        return carry
+
+    lax.fori_loop(1, devices, greet, 0)
 
     def lay_out(node):
         branch[node * size:(node + 1) * size, :] = jnp.broadcast_to(matrices[:, node:node + 1], (size, 128))
@@ -166,7 +172,7 @@
             store_root(entries, w, scale[w])
 
         if turn == 0:
-            pl.semaphore_wait(barrier, clades - 1 + sites_axis - 1)
+            pl.semaphore_wait(barrier, devices - 1)
         for step in range(turn, half_clades):
             target = half * half_clades + lax.rem(my_low + step, half_clades)
             slot = turn * half_clades + step
@@ -196,28 +202,31 @@
     value = weights[me].astype(jnp.float32) * (jnp.log(summed) + scale) / float(leaves * clades)
     weighted[...] = value
 
-    def exchange(axis, index, count, sums, send, recv, mine):
-        sums[index] = mine
-        copies = []
-        for step in range(1, count):
-            copy = pltpu.make_async_remote_copy(
-                src_ref=sums.at[index], dst_ref=sums.at[index],
-                send_sem=send.at[step], recv_sem=recv.at[step],
-                device_id={axis: lax.rem(index + step, count)}, device_id_type=MESH)
-            copy.start()
-            copies.append(copy)
-        for copy in copies:
-            copy.wait_recv()
-        return copies, tree_sum([sums[k] for k in range(count)])
-
-    copies, total = exchange("clade", me, clades, sums_clade, clade_send, clade_recv,
-                             jnp.sum(value, axis=0, keepdims=True))
-    root_copies += copies
-    copies, total = exchange("site", block, sites_axis, sums_site, site_send, site_recv, total)
-    root_copies += copies
-    mean[0] = jnp.sum(total) / float(rows * 128 * sites_axis)
+    sums[mine] = jnp.sum(value, axis=0, keepdims=True)
+
+    def send_sum(step, carry):
+        other = lax.rem(mine + step, devices)
+        pltpu.make_async_remote_copy(
+            src_ref=sums.at[mine], dst_ref=sums.at[mine], send_sem=sum_send, recv_sem=sum_recv,
+            device_id={"site": other // clades, "clade": lax.rem(other, clades)}, device_id_type=MESH).start()
+        return carry
+
+    lax.fori_loop(1, devices, send_sum, 0)
+    everyone = pltpu.make_async_remote_copy(
+        src_ref=sums.at[pl.ds(1, devices - 1)], dst_ref=sums.at[pl.ds(1, devices - 1)],
+        send_sem=sum_send, recv_sem=sum_recv, device_id={"clade": lax.rem(me + 1, clades)}, device_id_type=MESH)
+    everyone.wait_recv()
+    mean[...] = tree_sum([sums[k] for k in range(devices)])
+    everyone.wait_send()
     for copy in root_copies:
         copy.wait_send()
+
+
+def finish(sites, value, total, weighted, mean, sem):
+    copy = pltpu.make_async_copy(value, weighted, sem)
+    copy.start()
+    mean[0] = jnp.sum(total[...]) / sites
+    copy.wait()
 
 
 def per_device(tips, transition, clade_children, upper_transition, upper_children, pattern_weights):
@@ -237,9 +246,9 @@
     smem = pl.BlockSpec(memory_space=pltpu.SMEM)
     weighted, mean = pl.pallas_call(
         functools.partial(kernel, (leaves, rates, rows, clades, sites_axis)),
-        out_shape=(jax.ShapeDtypeStruct((piece, 128), jnp.float32), jax.ShapeDtypeStruct((1,), jnp.float32)),
+        out_shape=(pltpu.VMEM((piece, 128), jnp.float32), pltpu.VMEM((1, 128), jnp.float32)),
         in_specs=[pl.BlockSpec(memory_space=pltpu.HBM)] * 6,
-        out_specs=(vmem, smem),
+        out_specs=(vmem, vmem),
         scratch_shapes=[
             pltpu.VMEM((2, leaves // 8, rows * 4, 128), jnp.int32),
             pltpu.VMEM((size, nodes), jnp.float32),
@@ -254,18 +263,22 @@
             pltpu.VMEM((nodes * entries, rows // 2, 128), jnp.float32),
             pltpu.VMEM((clades, entries + 1, piece, 128), jnp.float32),
             pltpu.VMEM((2 * clades - 2, entries + 1, piece, 128), jnp.float32),
-            pltpu.VMEM((clades, 1, 128), jnp.float32),
-            pltpu.VMEM((sites_axis, 1, 128), jnp.float32),
+            pltpu.VMEM((clades * sites_axis, 1, 128), jnp.float32),
             pltpu.SemaphoreType.DMA((clades,)),
             pltpu.SemaphoreType.DMA((clades,)),
-            pltpu.SemaphoreType.DMA((clades,)),
-            pltpu.SemaphoreType.DMA((clades,)),
-            pltpu.SemaphoreType.DMA((sites_axis,)),
-            pltpu.SemaphoreType.DMA((sites_axis,)),
+            pltpu.SemaphoreType.DMA,
+            pltpu.SemaphoreType.DMA,
         ],
         compiler_params=pltpu.CompilerParams(
-            collective_id=0, has_side_effects=True, vmem_limit_bytes=67043328),
+            collective_id=0, has_side_effects=True, vmem_limit_bytes=67043328 - 16384),
     )(codes, matrices, clade_children.T, upper, upper_children.T, pattern_weights.reshape(clades, piece, 128))
+    weighted, mean = pl.pallas_call(
+        functools.partial(finish, float(sites * sites_axis)),
+        out_shape=(jax.ShapeDtypeStruct((piece, 128), jnp.float32), jax.ShapeDtypeStruct((1,), jnp.float32)),
+        in_specs=[vmem, vmem],
+        out_specs=(pl.BlockSpec(memory_space=pltpu.HBM), smem),
+        scratch_shapes=[pltpu.SemaphoreType.DMA],
+    )(pltpu.with_memory_space_constraint(weighted, pltpu.VMEM), pltpu.with_memory_space_constraint(mean, pltpu.VMEM))
     return weighted.reshape(sites // clades), mean.reshape(())
 
 

time: 23 us -> 18.1 us (0.79)
  Pallas kernels: 19.1 us -> 17.3 us
  between operations: 2.41 us -> 0.64 us
  local copies, waits for them, and re-layouts: 1.26 us -> 0 us
    pallas_call x1, Pallas kernels: 19.1 us -> 16.2 us  [per_device(): pl.pallas_call(functools.partial(kernel, (leaves, rates, rows, clades, si...]
    unnamed x3 -> x0, local copies, waits for them, and re-layouts: 1.26 us -> none
    pallas_call x0 -> x1, Pallas kernels: none -> 1.12 us  [per_device(): pl.pallas_call(functools.partial(finish, float(sites * sites_axis)), out_...]
where the time goes in v1:
time: 18.1 us; the launch traced here: 17.9 us
  Pallas kernels  17.3 us (96%)
  between operations  0.64 us (4%)
    pallas_call x1, Pallas kernels, per_device(): pl.pallas_call(functools.partial(kernel, (leaves, rates, rows, clades, si...  16.2 us
    pallas_call x1, Pallas kernels, per_device(): pl.pallas_call(functools.partial(finish, float(sites * sites_axis)), out_...  1.12 us

profile of v1, /device:TPU:0, one launch (start us, length us, event | category | flops | bytes accessed | tf_op | source)
XLA Modules:
  0.0 17.9 jit_solution(9807305191689617687)
XLA Ops:
  0.6 16.2 %shard_map.77 = (f32[8,128]{1,0:T(8,128)S(1)}, f32[1,128]{1,0:T(1,128)S(1)}) custom-call(s32[4,256,128]{2,1,0:T(8,128)} %bitcast.16, f32[64,62]{1,0:T(8,128)} %bitcast.17, s32[2,31]{1,0:T(2,128)} %bitcast.20, f32[64,6]{1,0:T(8,128)} %bitcast.18, s32[2,3]{1,0:T(2,128)} %bitcast.21, s32[4,8,128]{2,1,0:T(8,128)} %bitcast.19), custom_call_target="tpu_custom_call" | custom-call | tf_op jit(solution)/shard_map/pallas_call | solution.py:247
  16.8 1.1 %shard_map.78 = (f32[8,128]{1,0:T(8,128)}, f32[1]{0:T(128)}) custom-call(f32[8,128]{1,0:T(8,128)S(1)} %get-tuple-element.6.value, f32[1,128]{1,0:T(1,128)S(1)} %get-tuple-element.7.total), custom_call_target="tpu_custom_call" | custom-call | tf_op jit(solution)/shard_map/pallas_call | solution.py:275

commit v2 on v1

v2 whole, which is shorter than its diff:
```python
import functools

import jax
import jax.numpy as jnp
from jax import lax
from jax.experimental import pallas as pl
from jax.experimental.pallas import tpu as pltpu
from jax.sharding import PartitionSpec as P

MESH = pl.DeviceIdType.MESH
UNROLL = True
EARLY = 10
LATER = [[1], [2], []]


def tree_max(values):
    while len(values) > 1:
        paired = [jnp.maximum(a, b) for a, b in zip(values[::2], values[1::2])]
        values = paired + ([values[-1]] if len(values) % 2 else [])
    return values[0]


def tree_sum(values):
    while len(values) > 1:
        paired = [a + b for a, b in zip(values[::2], values[1::2])]
        values = paired + ([values[-1]] if len(values) % 2 else [])
    return values[0]


def look_up(table, code):
    dims = lax.GatherDimensionNumbers(
        offset_dims=(), collapsed_slice_dims=(0,), start_index_map=(0,),
        operand_batching_dims=(1,), start_indices_batching_dims=(1,))
    return lax.gather(table, code[..., None], dims, slice_sizes=(1, 1), mode=lax.GatherScatterMode.PROMISE_IN_BOUNDS)


def kernel(dims, tips_in, matrices_in, children_in, upper_in, upper_children_in, weights_in,
           weighted, mean, tips, matrices, children, upper, upper_children, weights, load,
           tables, branch, upper_branch, root, held, sums,
           root_send, root_recv, sum_send, sum_recv, here, *moved):
    leaves, rates, rows, clades, sites_axis = dims
    entries = rates * 4
    size = entries * 4
    nodes = 2 * leaves - 2
    inner = leaves - 1
    piece = rows // clades
    shares = 8 // piece
    windows = rows // 8
    near = windows // 2
    me = lax.axis_index("clade")
    block = lax.axis_index("site")
    devices = clades * sites_axis
    mine = block * clades + me
    own = me // shares
    my_share = lax.rem(me, shares)
    half, low = own // near, lax.rem(own, near)
    order = [(1 - half) * near + lax.rem(low + s, near) for s in range(near)]
    order += [half * near + lax.rem(low + s + 1, near) for s in range(near)]
    groups = [[t] for t in range(near)] + [list(range(near, windows))]

    def tips_start(turn):
        for k in range(leaves // 8):
            pltpu.make_async_copy(tips_in.at[k, pl.ds(order[turn] * 64, 64), :], tips.at[turn, k],
                                  load.at[0 if turn == 0 else 1]).start()

    def tips_wait(start, stop):
        span = tips.at[pl.ds(start, stop - start)]
        pltpu.make_async_copy(span, span, load.at[0 if start == 0 else 1]).wait()

    loads = [pltpu.make_async_copy(source, target, load.at[2 + k]) for k, (source, target) in enumerate([
        (matrices_in, matrices), (children_in, children), (upper_in, upper),
        (upper_children_in, upper_children), (weights_in, weights)])]
    loads[0].start()
    tips_start(0)
    for copy in loads[1:]:
        copy.start()
    for turn in range(1, windows):
        tips_start(turn)

    barrier = pltpu.get_barrier_semaphore()

    def to_site(index):
        return {"site": index // clades, "clade": lax.rem(index, clades)}

    for step in range(1, clades):
        pl.semaphore_signal(barrier, inc=1, device_id={"clade": lax.rem(me + step, clades)}, device_id_type=MESH)

    def greet(other, carry):
        pl.semaphore_signal(barrier, inc=1, device_id=to_site(other), device_id_type=MESH)
        return carry

    lax.fori_loop((block + 1) * clades, devices, greet, 0)

    loads[0].wait()
    first = lax.broadcasted_iota(jnp.int32, (8, 128), 0) < 4

    def lay_out(node):
        branch[node * size:(node + 1) * size, :] = jnp.broadcast_to(
            matrices[:, leaves + node:leaves + node + 1], (size, 128))

    def tip_codes(turn, i):
        return tips[turn, i // 8, pl.ds(lax.rem(i, 8), 8, stride=8), :]

    def tip_rest(i, targets):
        codes = {turn: tip_codes(turn, i) for group in targets for turn in groups[group]}
        for entry in range(entries):
            table = tables[i * entries + entry]
            for group in targets:
                for w, turn in enumerate(groups[group]):
                    moved[group][i * entries + entry, w * 8:(w + 1) * 8, :] = look_up(table, codes[turn])

    def tip_tables(i):
        for pair in range(entries // 2):
            both = jnp.broadcast_to(matrices[pair * 8:pair * 8 + 8, i:i + 1], (8, 128))
            tables[i * entries + 2 * pair] = jnp.where(first, both, 1.0)
            tables[i * entries + 2 * pair + 1] = jnp.where(first, pltpu.roll(both, 4, 0), 1.0)

    for i in range(EARLY):
        tip_tables(i)
    tips_wait(0, 1)
    for i in range(leaves):
        if i + EARLY < leaves:
            tip_tables(i + EARLY)
        tip_rest(i, [0])
        if not UNROLL and i < inner - 1:
            lay_out(i)
    loads[1].wait()
    tips_wait(1, windows)
    loads[2].wait()
    for node in range(2 * clades - 2):
        upper_branch[node * size:(node + 1) * size, :] = jnp.broadcast_to(upper[:, node:node + 1], (size, 128))

    def spread(ref, row, count=8):
        return jnp.broadcast_to(ref[pl.ds(row, 1), :], (count, 128))

    def merge(left, right):
        product = [a * b for a, b in zip(left, right)]
        biggest = tree_max(product)
        inverse = 1.0 / biggest
        return [p * inverse for p in product], jnp.log(biggest)

    def transform(ref, base, parts, store):
        count = parts[0][0].shape[0]
        for rate in range(rates):
            for state in range(4):
                entry = rate * 4 + state
                acc = None
                for b in range(4):
                    weight = spread(ref, base + entry * 4 + b, count)
                    terms = [weight * part[rate * 4 + b] for part in parts]
                    acc = terms if acc is None else [x + y for x, y in zip(acc, terms)]
                for w, value in enumerate(acc):
                    store(entry, w, value)

    def rows_of(j):
        return children[0, j] * entries, children[1, j] * entries

    for index, (group, target) in enumerate(zip(groups, moved)):
        width = len(group)

        def merged(c, d, scale):
            parts, scales = [], []
            for w in range(width):
                window = slice(w * 8, (w + 1) * 8)
                part, log_m = merge([target[c + e, window, :] for e in range(entries)],
                                    [target[d + e, window, :] for e in range(entries)])
                parts.append(part)
                scales.append(scale[w] + log_m)
            return parts, tuple(scales)

        def advance(j, carry):
            c, d, scale = carry
            after = rows_of(j + 1)
            if UNROLL and index == 0:
                lay_out(j)
            parts, scale = merged(c, d, scale)

            def store(entry, w, value):
                target[(leaves + j) * entries + entry, w * 8:(w + 1) * 8, :] = value

            transform(branch, j * size, parts, store)
            if later:
                tip_rest(j + leaves - inner + 1, later)
            return *after, scale

        later = LATER[index]
        if later:
            for i in range(leaves - inner + 1):
                tip_rest(i, later)
        carry = *rows_of(0), tuple(jnp.zeros((8, 128), jnp.float32) for _ in group)
        if UNROLL and index == 0:
            for j in range(inner - 1):
                carry = advance(j, carry)
        else:
            carry = lax.fori_loop(0, inner - 1, advance, carry)
        parts, scale = merged(*carry)

        def store_root(entry, w, value):
            for k in range(shares):
                root[group[w], k, entry] = value[k * piece:(k + 1) * piece, :]

        transform(upper_branch, me * size, parts, store_root)
        for w in range(width):
            store_root(entries, w, scale[w])

        if index == 0:
            pl.semaphore_wait(barrier, clades - 1 + block * clades)
        for turn in group:
            for k in range(shares):
                if turn < windows - 1:
                    share = k
                elif k:
                    share = lax.rem(my_share + k, shares)
                else:
                    continue
                pltpu.make_async_remote_copy(
                    src_ref=root.at[turn, share], dst_ref=held.at[me], send_sem=root_send, recv_sem=root_recv,
                    device_id={"clade": order[turn] * shares + share}, device_id_type=MESH).start()
        if index == len(groups) - 2:
            def answer(other, carry):
                pl.semaphore_signal(here, inc=1, device_id={"site": other}, device_id_type=MESH)
                return carry

            lax.fori_loop(0, block, answer, 0)

    held[me] = root[windows - 1, my_share]
    roots = pltpu.make_async_remote_copy(
        src_ref=held.at[pl.ds(0, clades - 1)], dst_ref=held.at[pl.ds(0, clades - 1)],
        send_sem=root_send, recv_sem=root_recv, device_id={"clade": lax.rem(me + 1, clades)}, device_id_type=MESH)
    loads[3].wait()
    loads[4].wait()
    roots.wait_recv()

    scale = tree_sum([held[k, entries] for k in range(clades)])
    for j in range(clades - 1):
        c = upper_children[0, j]
        d = upper_children[1, j]
        part, log_m = merge([held[c, e] for e in range(entries)], [held[d, e] for e in range(entries)])
        scale = scale + log_m
        if j < clades - 2:
            def store_upper(entry, w, value):
                held[clades + j, entry, :, :] = value

            transform(upper_branch, (clades + j) * size, [part], store_upper)
    summed = tree_sum(part) / (4.0 * rates)
    value = weights[me].astype(jnp.float32) * (jnp.log(summed) + scale) / float(leaves * clades)
    weighted[...] = value

    sums[mine] = jnp.sum(value, axis=0, keepdims=True)

    def send_sum(other, carry):
        pltpu.make_async_remote_copy(
            src_ref=sums.at[mine], dst_ref=sums.at[mine], send_sem=sum_send, recv_sem=sum_recv,
            device_id=to_site(other), device_id_type=MESH).start()
        return carry

    lax.fori_loop(0, block * clades, send_sum, 0)
    for step in range(1, clades):
        send_sum(block * clades + lax.rem(me + step, clades), 0)

    @pl.when(block < sites_axis - 1)
    def _():
        pl.semaphore_wait(here, sites_axis - 1 - block)

    lax.fori_loop((block + 1) * clades, devices, send_sum, 0)
    everyone = pltpu.make_async_remote_copy(
        src_ref=sums.at[pl.ds(1, devices - 1)], dst_ref=sums.at[pl.ds(1, devices - 1)],
        send_sem=sum_send, recv_sem=sum_recv, device_id={"clade": lax.rem(me + 1, clades)}, device_id_type=MESH)
    roots.wait_send()
    everyone.wait_send()
    everyone.wait_recv()
    mean[...] = tree_sum([sums[k] for k in range(devices)])


def finish(sites, value, total, weighted, mean, sem):
    copy = pltpu.make_async_copy(value, weighted, sem)
    copy.start()
    mean[0] = jnp.sum(total[...]) / sites
    copy.wait()


def per_device(tips, transition, clade_children, upper_transition, upper_children, pattern_weights):
    leaves, sites = tips.shape
    rates = transition.shape[1]
    clades = lax.axis_size("clade")
    sites_axis = lax.axis_size("site")
    rows = sites // 128
    piece = rows // clades
    windows = rows // 8
    near = windows // 2
    entries = rates * 4
    size = entries * 4
    nodes = 2 * leaves - 2
    codes = tips.reshape(leaves // 8, 8, rows, 128).transpose(0, 2, 1, 3).reshape(leaves // 8, rows * 8, 128)
    matrices = transition.transpose(1, 2, 3, 0).reshape(size, nodes)
    upper = upper_transition.transpose(1, 2, 3, 0).reshape(size, 2 * clades - 2)
    vmem = pl.BlockSpec(memory_space=pltpu.VMEM)
    smem = pl.BlockSpec(memory_space=pltpu.SMEM)
    weighted, mean = pl.pallas_call(
        functools.partial(kernel, (leaves, rates, rows, clades, sites_axis)),
        out_shape=(pltpu.VMEM((piece, 128), jnp.float32), pltpu.VMEM((1, 128), jnp.float32)),
        in_specs=[pl.BlockSpec(memory_space=pltpu.HBM)] * 6,
        out_specs=(vmem, vmem),
        scratch_shapes=[
            pltpu.VMEM((windows, leaves // 8, 64, 128), jnp.int32),
            pltpu.VMEM((size, nodes), jnp.float32),
            pltpu.SMEM((2, leaves - 1), jnp.int32),
            pltpu.VMEM((size, 2 * clades - 2), jnp.float32),
            pltpu.SMEM((2, clades - 1), jnp.int32),
            pltpu.VMEM((clades, piece, 128), jnp.int32),
            pltpu.SemaphoreType.DMA((7,)),
            pltpu.VMEM((leaves * entries, 8, 128), jnp.float32),
            pltpu.VMEM(((leaves - 2) * size, 128), jnp.float32),
            pltpu.VMEM(((2 * clades - 2) * size, 128), jnp.float32),
            pltpu.VMEM((windows, 8 // piece, entries + 1, piece, 128), jnp.float32),
            pltpu.VMEM((2 * clades - 2, entries + 1, piece, 128), jnp.float32),
            pltpu.VMEM((clades * sites_axis, 1, 128), jnp.float32),
            pltpu.SemaphoreType.DMA,
            pltpu.SemaphoreType.DMA,
            pltpu.SemaphoreType.DMA,
            pltpu.SemaphoreType.DMA,
            pltpu.SemaphoreType.REGULAR,
        ] + [pltpu.VMEM((nodes * entries, 8 * width, 128), jnp.float32) for width in [1] * near + [windows - near]],
        compiler_params=pltpu.CompilerParams(
            collective_id=0, has_side_effects=True, vmem_limit_bytes=67043328 - 16384),
    )(codes, matrices, clade_children.T, upper, upper_children.T, pattern_weights.reshape(clades, piece, 128))
    weighted, mean = pl.pallas_call(
        functools.partial(finish, float(sites * sites_axis)),
        out_shape=(jax.ShapeDtypeStruct((piece, 128), jnp.float32), jax.ShapeDtypeStruct((1,), jnp.float32)),
        in_specs=[vmem, vmem],
        out_specs=(pl.BlockSpec(memory_space=pltpu.HBM), smem),
        scratch_shapes=[pltpu.SemaphoreType.DMA],
    )(pltpu.with_memory_space_constraint(weighted, pltpu.VMEM), pltpu.with_memory_space_constraint(mean, pltpu.VMEM))
    return weighted.reshape(sites // clades), mean.reshape(())


def solution(mesh):
    placed = (
        P("clade", "site"),
        P("clade", None, None, None),
        P("clade", None),
        P(),
        P(),
        P("site"),
    )
    return jax.shard_map(
        per_device,
        mesh=mesh,
        in_specs=placed,
        out_specs=(P(("site", "clade")), P()),
        check_vma=False,
    )
```

time: 18.1 us -> 17.3 us (0.956)
  Pallas kernels: 17.3 us -> 16.5 us
    pallas_call x1, Pallas kernels: 16.2 us -> 15.4 us  [per_device(): pl.pallas_call(functools.partial(kernel, (leaves, rates, rows, clades, si...]
where the time goes in v2:
time: 17.3 us; the launch traced here: 17.1 us
  Pallas kernels  16.5 us (95%)
  between operations  0.64 us (4%)
    pallas_call x1, Pallas kernels, per_device(): pl.pallas_call(functools.partial(kernel, (leaves, rates, rows, clades, si...  15.4 us
    pallas_call x1, Pallas kernels, per_device(): pl.pallas_call(functools.partial(finish, float(sites * sites_axis)), out_...  1.12 us

profile of v2, /device:TPU:0, one launch (start us, length us, event | category | flops | bytes accessed | tf_op | source)
XLA Modules:
  0.0 17.1 jit_solution(8072367393249107354)
XLA Ops:
  0.6 15.4 %shard_map.77 = (f32[8,128]{1,0:T(8,128)S(1)}, f32[1,128]{1,0:T(1,128)S(1)}) custom-call(s32[4,256,128]{2,1,0:T(8,128)} %bitcast.16, f32[64,62]{1,0:T(8,128)} %bitcast.17, s32[2,31]{1,0:T(2,128)} %bitcast.20, f32[64,6]{1,0:T(8,128)} %bitcast.18, s32[2,3]{1,0:T(2,128)} %bitcast.21, s32[4,8,128]{2,1,0:T(8,128)} %bitcast.19), custom_call_target="tpu_custom_call" | custom-call | tf_op jit(solution)/shard_map/pallas_call | solution.py:299
  16.0 1.1 %shard_map.78 = (f32[8,128]{1,0:T(8,128)}, f32[1]{0:T(128)}) custom-call(f32[8,128]{1,0:T(8,128)S(1)} %get-tuple-element.6.value, f32[1,128]{1,0:T(1,128)S(1)} %get-tuple-element.7.total), custom_call_target="tpu_custom_call" | custom-call | tf_op jit(solution)/shard_map/pallas_call | solution.py:327

commit v3 on v2

--- a/solution.py
+++ b/solution.py
@@ -8,9 +8,8 @@
 from jax.sharding import PartitionSpec as P
 
 MESH = pl.DeviceIdType.MESH
-UNROLL = True
 EARLY = 10
-LATER = [[1], [2], []]
+LAG = 22
 
 
 def tree_max(values):
@@ -54,27 +53,28 @@
     own = me // shares
     my_share = lax.rem(me, shares)
     half, low = own // near, lax.rem(own, near)
-    order = [(1 - half) * near + lax.rem(low + s, near) for s in range(near)]
+    order = [(1 - half) * near + s for s in range(near)]
     order += [half * near + lax.rem(low + s + 1, near) for s in range(near)]
-    groups = [[t] for t in range(near)] + [list(range(near, windows))]
+    groups = [[t] for t in range(windows)]
 
     def tips_start(turn):
         for k in range(leaves // 8):
             pltpu.make_async_copy(tips_in.at[k, pl.ds(order[turn] * 64, 64), :], tips.at[turn, k],
-                                  load.at[0 if turn == 0 else 1]).start()
+                                  load.at[turn // near]).start()
 
     def tips_wait(start, stop):
         span = tips.at[pl.ds(start, stop - start)]
-        pltpu.make_async_copy(span, span, load.at[0 if start == 0 else 1]).wait()
-
-    loads = [pltpu.make_async_copy(source, target, load.at[2 + k]) for k, (source, target) in enumerate([
-        (matrices_in, matrices), (children_in, children), (upper_in, upper),
-        (upper_children_in, upper_children), (weights_in, weights)])]
+        pltpu.make_async_copy(span, span, load.at[start // near]).wait()
+
+    loads = [pltpu.make_async_copy(source, target, load.at[k]) for k, source, target in [
+        (2, matrices_in, matrices), (3, children_in, children), (4, upper_in, upper),
+        (2, upper_children_in, upper_children), (3, weights_in, weights)]]
     loads[0].start()
-    tips_start(0)
-    for copy in loads[1:]:
+    for turn in range(near):
+        tips_start(turn)
+    for copy in loads[1:3]:
         copy.start()
-    for turn in range(1, windows):
+    for turn in range(near, windows):
         tips_start(turn)
 
     barrier = pltpu.get_barrier_semaphore()
@@ -92,6 +92,7 @@
     lax.fori_loop((block + 1) * clades, devices, greet, 0)
 
     loads[0].wait()
+    loads[3].start()
     first = lax.broadcasted_iota(jnp.int32, (8, 128), 0) < 4
 
     def lay_out(node):
@@ -117,15 +118,14 @@
 
     for i in range(EARLY):
         tip_tables(i)
-    tips_wait(0, 1)
+    tips_wait(0, near)
     for i in range(leaves):
         if i + EARLY < leaves:
             tip_tables(i + EARLY)
-        tip_rest(i, [0])
-        if not UNROLL and i < inner - 1:
-            lay_out(i)
+        tip_rest(i, [0, 1])
     loads[1].wait()
-    tips_wait(1, windows)
+    loads[4].start()
+    tips_wait(near, windows)
     loads[2].wait()
     for node in range(2 * clades - 2):
         upper_branch[node * size:(node + 1) * size, :] = jnp.broadcast_to(upper[:, node:node + 1], (size, 128))
@@ -155,72 +155,71 @@
     def rows_of(j):
         return children[0, j] * entries, children[1, j] * entries
 
-    for index, (group, target) in enumerate(zip(groups, moved)):
-        width = len(group)
-
-        def merged(c, d, scale):
-            parts, scales = [], []
-            for w in range(width):
-                window = slice(w * 8, (w + 1) * 8)
-                part, log_m = merge([target[c + e, window, :] for e in range(entries)],
-                                    [target[d + e, window, :] for e in range(entries)])
-                parts.append(part)
-                scales.append(scale[w] + log_m)
-            return parts, tuple(scales)
-
-        def advance(j, carry):
-            c, d, scale = carry
-            after = rows_of(j + 1)
-            if UNROLL and index == 0:
-                lay_out(j)
-            parts, scale = merged(c, d, scale)
-
+    def answer(other, carry):
+        pl.semaphore_signal(here, inc=1, device_id={"site": other}, device_id_type=MESH)
+        return carry
+
+    class Walk:
+        def __init__(self, turn):
+            self.turn, self.rows, self.scale = turn, moved[turn], 0.0
+
+        def take(self, j):
+            c, d = rows_of(j)
+            self.part, log_m = merge([self.rows[c + e] for e in range(entries)],
+                                     [self.rows[d + e] for e in range(entries)])
+            self.scale = self.scale + log_m
+
+        def put(self, j):
             def store(entry, w, value):
-                target[(leaves + j) * entries + entry, w * 8:(w + 1) * 8, :] = value
-
-            transform(branch, j * size, parts, store)
-            if later:
-                tip_rest(j + leaves - inner + 1, later)
-            return *after, scale
-
-        later = LATER[index]
-        if later:
-            for i in range(leaves - inner + 1):
-                tip_rest(i, later)
-        carry = *rows_of(0), tuple(jnp.zeros((8, 128), jnp.float32) for _ in group)
-        if UNROLL and index == 0:
-            for j in range(inner - 1):
-                carry = advance(j, carry)
-        else:
-            carry = lax.fori_loop(0, inner - 1, advance, carry)
-        parts, scale = merged(*carry)
-
-        def store_root(entry, w, value):
+                self.rows[(leaves + j) * entries + entry] = value
+
+            transform(branch, j * size, [self.part], store)
+
+        def finish(self):
+            def store(entry, w, value):
+                for k in range(shares):
+                    root[self.turn, k, entry] = value[k * piece:(k + 1) * piece, :]
+
+            transform(upper_branch, me * size, [self.part], store)
+            store(entries, 0, self.scale)
+            if self.turn == 0:
+                pl.semaphore_wait(barrier, clades - 1 + block * clades)
             for k in range(shares):
-                root[group[w], k, entry] = value[k * piece:(k + 1) * piece, :]
-
-        transform(upper_branch, me * size, parts, store_root)
-        for w in range(width):
-            store_root(entries, w, scale[w])
-
-        if index == 0:
-            pl.semaphore_wait(barrier, clades - 1 + block * clades)
-        for turn in group:
-            for k in range(shares):
-                if turn < windows - 1:
+                if self.turn < windows - 1:
                     share = k
                 elif k:
                     share = lax.rem(my_share + k, shares)
                 else:
                     continue
                 pltpu.make_async_remote_copy(
-                    src_ref=root.at[turn, share], dst_ref=held.at[me], send_sem=root_send, recv_sem=root_recv,
-                    device_id={"clade": order[turn] * shares + share}, device_id_type=MESH).start()
-        if index == len(groups) - 2:
-            def answer(other, carry):
-                pl.semaphore_signal(here, inc=1, device_id={"site": other}, device_id_type=MESH)
-                return carry
-
+                    src_ref=root.at[self.turn, share], dst_ref=held.at[me], send_sem=root_send, recv_sem=root_recv,
+                    device_id={"clade": order[self.turn] * shares + share}, device_id_type=MESH).start()
+
+    for pair in range(0, windows, 2):
+        ahead, behind = Walk(pair), Walk(pair + 1)
+        later = list(range(pair + 2, min(pair + 4, windows)))
+        pending = iter(range(leaves))
+        for step in range(inner + LAG):
+            alone = step >= inner
+            if not alone:
+                ahead.take(step)
+            if 0 < step - LAG:
+                behind.put(step - LAG - 1)
+            if step < inner - 1:
+                if pair == 0:
+                    lay_out(step)
+                ahead.put(step)
+            if step == inner - 1:
+                ahead.finish()
+            if step >= LAG:
+                behind.take(step - LAG)
+            if alone and later:
+                for i in range(-(-leaves // LAG)):
+                    tip = next(pending, None)
+                    if tip is not None:
+                        tip_rest(tip, later)
+        behind.finish()
+        if pair == 0:
             lax.fori_loop(0, block, answer, 0)
 
     held[me] = root[windows - 1, my_share]
@@ -308,7 +307,7 @@
             pltpu.VMEM((size, 2 * clades - 2), jnp.float32),
             pltpu.SMEM((2, clades - 1), jnp.int32),
             pltpu.VMEM((clades, piece, 128), jnp.int32),
-            pltpu.SemaphoreType.DMA((7,)),
+            pltpu.SemaphoreType.DMA((5,)),
             pltpu.VMEM((leaves * entries, 8, 128), jnp.float32),
             pltpu.VMEM(((leaves - 2) * size, 128), jnp.float32),
             pltpu.VMEM(((2 * clades - 2) * size, 128), jnp.float32),
@@ -320,7 +319,7 @@
             pltpu.SemaphoreType.DMA,
             pltpu.SemaphoreType.DMA,
             pltpu.SemaphoreType.REGULAR,
-        ] + [pltpu.VMEM((nodes * entries, 8 * width, 128), jnp.float32) for width in [1] * near + [windows - near]],
+        ] + [pltpu.VMEM((nodes * entries, 8, 128), jnp.float32) for _ in range(windows)],
         compiler_params=pltpu.CompilerParams(
             collective_id=0, has_side_effects=True, vmem_limit_bytes=67043328 - 16384),
     )(codes, matrices, clade_children.T, upper, upper_children.T, pattern_weights.reshape(clades, piece, 128))

time: 17.3 us -> 16.9 us (0.977)
  Pallas kernels: 16.5 us -> 16.1 us
    pallas_call x1, Pallas kernels: 15.4 us -> 14.9 us  [per_device(): pl.pallas_call(functools.partial(kernel, (leaves, rates, rows, clades, si...]
where the time goes in v3:
time: 16.9 us; the launch traced here: 16.7 us
  Pallas kernels  16.1 us (95%)
  between operations  0.64 us (4%)
    pallas_call x1, Pallas kernels, per_device(): pl.pallas_call(functools.partial(kernel, (leaves, rates, rows, clades, si...  14.9 us
    pallas_call x1, Pallas kernels, per_device(): pl.pallas_call(functools.partial(finish, float(sites * sites_axis)), out_...  1.12 us

profile of v3, /device:TPU:0, one launch (start us, length us, event | category | flops | bytes accessed | tf_op | source)
XLA Modules:
  0.0 16.7 jit_solution(16237188489353567699)
XLA Ops:
  0.6 14.9 %shard_map.77 = (f32[8,128]{1,0:T(8,128)S(1)}, f32[1,128]{1,0:T(1,128)S(1)}) custom-call(s32[4,256,128]{2,1,0:T(8,128)} %bitcast.16, f32[64,62]{1,0:T(8,128)} %bitcast.17, s32[2,31]{1,0:T(2,128)} %bitcast.20, f32[64,6]{1,0:T(8,128)} %bitcast.18, s32[2,3]{1,0:T(2,128)} %bitcast.21, s32[4,8,128]{2,1,0:T(8,128)} %bitcast.19), custom_call_target="tpu_custom_call" | custom-call | tf_op jit(solution)/shard_map/pallas_call | solution.py:298
  15.6 1.1 %shard_map.78 = (f32[8,128]{1,0:T(8,128)}, f32[1]{0:T(128)}) custom-call(f32[8,128]{1,0:T(8,128)S(1)} %get-tuple-element.6.value, f32[1,128]{1,0:T(1,128)S(1)} %get-tuple-element.7.total), custom_call_target="tpu_custom_call" | custom-call | tf_op jit(solution)/shard_map/pallas_call | solution.py:326
